TPU v7x, 256 devices: a 2x2x32 block of a 4x8x32 slice. The times are simulated.
256 devices in a mesh: image: 4 (over y, x), row: 64 (over z, core).
Axes of the slice: x: 2, y: 2, z: 32, core: 2. Of those that a mesh axis runs over, the one named last changes fastest.
The devices are a block of a 4x8x32 slice.
Arguments:
- density: float32 [2048, 7, 128, 128], P(('image', 'row')), parts along dimension 0, as said below
- block_columns: int32 [2048, 7], P(('image', 'row')), parts along dimension 0, may hold values from -1 to 511, as said below
Outputs:
- purified: float32 [2048, 7, 128, 128], P(('image', 'row')), parts along dimension 0
- occupation: float32 [12], P('image'), parts along dimension 0
There are 4 independent parts, one for each index of `image`. A program takes and returns all parts, laid end to end along the dimension named above; each array names one. Nothing has to cross between parts.
Inputs may be any that keep to these rules, and one draw needn't show every extreme that they name: `block_columns`: slot s of block row i holds block column i - 3 + s or is empty (-1); slot 3 (column i) is never empty, and no slot points outside the matrix; the pattern is symmetric (j is in row i exactly when i is in row j); every draw has rows with all 7 slots filled. The density matrix is symmetric: the block in slot s of row i is the transpose of the block of row j = block_columns[i, s] whose column is i, and every diagonal block is symmetric.
All inputs are finite; a program needn't handle non-finite values.
Results may differ from a plain program's by a relative error of at most 0.0003.
Values sent between devices are 32-bit elements; how exact they have to be, the bound alone decides.
No kernel may reach another device: no remote copies, remote signals or barrier semaphores. Data moves between devices by JAX's collectives and lax.ppermute only.
A program may use at most 128 MiB of HBM per device.

v0:
```python
import functools

import jax
import jax.numpy as jnp
from jax import lax
from jax.experimental import pallas as pl
from jax.experimental.pallas import tpu as pltpu
from jax.sharding import PartitionSpec as P

HALF = 3
STEPS = 2
PAD = 4
TRIANGLE = [(a, b) for a in range(HALF) for b in range(a, HALF)]


def low_edge():
    return [(a, s) for a in range(HALF) for s in range(0, 2 * HALF - a)]


def high_edge(rows):
    return [(rows - HALF + a, s) for a in range(HALF) for s in range(HALF - a, 2 * HALF + 1)]


def split(value):
    high = value.astype(jnp.bfloat16)
    return high, (value - high.astype(jnp.float32)).astype(jnp.bfloat16)


def edge_kernel(columns_ref, *refs):
    blocks, outs = refs[: 4 * HALF], refs[4 * HALF :]
    rows = columns_ref.shape[0]
    for side, (out, base) in enumerate(zip(outs, (0, rows - HALF))):
        for n, (a, b) in enumerate(TRIANGLE):
            keep = (columns_ref[base + a, HALF + b - a] >= 0).astype(jnp.float32)
            out[n] = blocks[side * len(TRIANGLE) + n][0, 0] * keep


def edges(density, columns):
    rows, _, size, _ = density.shape
    picks = [(base + a, HALF + b - a) for base in (0, rows - HALF) for a, b in TRIANGLE]
    shape = jax.ShapeDtypeStruct((len(TRIANGLE), size, size), jnp.float32)
    specs = [pl.BlockSpec((1, 1, size, size), lambda g, r=r, s=s: (r, s, 0, 0)) for r, s in picks]
    whole = pl.BlockSpec((len(TRIANGLE), size, size), lambda g: (0, 0, 0))
    return pl.pallas_call(
        edge_kernel,
        grid=(1,),
        in_specs=[pl.BlockSpec(memory_space=pltpu.SMEM)] + specs,
        out_specs=[whole, whole],
        out_shape=[shape, shape],
        name="edges",
    )(columns, *([density] * len(picks)))


def diagonal_lanes(block):
    size = block.shape[0]
    eye = lax.broadcasted_iota(jnp.int32, (size, size), 0) == lax.broadcasted_iota(jnp.int32, (size, size), 1)
    return jnp.sum(jnp.where(eye, block, 0.0), axis=0, keepdims=True)


def step_kernel(first, columns_ref, p_ref, before_ref, after_ref, out_ref, *rest):
    rows, slots, size, _ = p_ref.shape
    window = rows + 2 * PAD
    if first:
        low_ref, high_ref, trace_ref, dh, dl, sh, sl = rest
    else:
        trace_ref, dh, dl, sh, sl = rest

    def keep(i, s):
        return (columns_ref[i, s] >= 0).astype(jnp.float32)

    def area(ref, p, q):
        return ref.at[p * size : (p + 1) * size, q * size : (q + 1) * size]

    def put(p, q, value):
        high, low = split(value)
        area(dh, p, q)[...] = high
        area(dl, p, q)[...] = low

    filled = set()
    old_trace = jnp.zeros((1, size), jnp.float32)
    for i in range(rows):
        for s in range(slots):
            block = p_ref[i, s]
            if first:
                block = block * keep(i, s)
            if s == HALF:
                old_trace += diagonal_lanes(block)
            p, q = PAD + i, PAD + i + s - HALF
            put(p, q, block)
            filled.add((p, q))
            if first and not PAD <= q < PAD + rows:
                put(q, p, block.T)
                filled.add((q, p))
    if first:
        for ref, base in ((before_ref, PAD - HALF), (after_ref, PAD + rows)):
            for n, (a, b) in enumerate(TRIANGLE):
                block = ref[n]
                put(base + a, base + b, block)
                filled.add((base + a, base + b))
                if a != b:
                    put(base + b, base + a, block.T)
                    filled.add((base + b, base + a))
    else:
        for ref, picks, shift in (
            (before_ref, high_edge(rows), PAD - rows),
            (after_ref, low_edge(), PAD + rows),
        ):
            for n, (i, s) in enumerate(picks):
                p = i + shift
                put(p, p + s - HALF, ref[n])
                filled.add((p, p + s - HALF))
    zero = jnp.zeros((size, size), jnp.bfloat16)
    for p in range(window):
        for q in range(window):
            if abs(p // 2 - q // 2) <= 2 and (p, q) not in filled:
                area(dh, p, q)[...] = zero
                area(dl, p, q)[...] = zero
    for i in range(rows):
        for q in range(window):
            if abs((PAD + i) // 2 - q // 2) <= 2 and abs(PAD + i - q) > HALF:
                area(sh, i, q)[...] = zero
                area(sl, i, q)[...] = zero

    def product(xh, xl, shift, write):
        for i in range(rows):
            p = PAD + i
            first_pair, last_pair = (p - HALF) // 2, (p + HALF) // 2
            for pair in range(first_pair, last_pair + 1):
                j0, j1 = max(first_pair, pair - 2), min(last_pair, pair + 2)
                if 2 * pair + 1 < p - HALF + 1:
                    j1 = min(j1, (2 * pair + 1 + HALF) // 2)
                if 2 * pair > p + HALF - 1:
                    j0 = max(j0, (2 * pair - HALF) // 2)
                inner = slice(2 * j0 * size, 2 * (j1 + 1) * size)
                across = slice(2 * pair * size, 2 * (pair + 1) * size)
                mine = slice((i + shift) * size, (i + shift + 1) * size)
                ah, al = xh[mine, inner], xl[mine, inner]
                bh, bl = dh[inner, across], dl[inner, across]
                dot = functools.partial(jnp.dot, preferred_element_type=jnp.float32)
                total = dot(ah, bh) + dot(ah, bl) + dot(al, bh)
                for half in range(2):
                    s = 2 * pair + half - p + HALF
                    if 0 <= s < slots:
                        write(i, s, total[:, half * size : (half + 1) * size] * keep(i, s))

    def write_square(i, s, block):
        out_ref[i, s] = block
        high, low = split(block)
        area(sh, i, PAD + i + s - HALF)[...] = high
        area(sl, i, PAD + i + s - HALF)[...] = low

    product(dh, dl, PAD, write_square)
    traces = []

    def write_next(i, s, cube):
        block = 3.0 * out_ref[i, s] - 2.0 * cube
        out_ref[i, s] = block
        if s == HALF:
            traces.append(diagonal_lanes(block))
        if first:
            for ref, picks in ((low_ref, low_edge()), (high_ref, high_edge(rows))):
                if (i, s) in picks:
                    ref[picks.index((i, s))] = block

    product(sh, sl, 0, write_next)
    new_trace = sum(traces[1:], traces[0])
    trace_ref[...] = jnp.zeros(trace_ref.shape, jnp.float32)
    if first:
        trace_ref[0:1, :] = old_trace
        trace_ref[1:2, :] = new_trace
    else:
        trace_ref[2:3, :] = new_trace


def step(first, columns, current, before, after):
    rows, slots, size, _ = current.shape
    window = rows + 2 * PAD
    f32 = jnp.float32
    outs = [jax.ShapeDtypeStruct(current.shape, f32)]
    if first:
        outs += [jax.ShapeDtypeStruct((len(low_edge()), size, size), f32)] * 2
    outs += [jax.ShapeDtypeStruct((8, size), f32)]
    vmem = pl.BlockSpec(memory_space=pltpu.VMEM)
    return pl.pallas_call(
        functools.partial(step_kernel, first),
        in_specs=[pl.BlockSpec(memory_space=pltpu.SMEM), vmem, vmem, vmem],
        out_specs=[vmem] * len(outs),
        out_shape=outs,
        scratch_shapes=[pltpu.VMEM((window * size, window * size), jnp.bfloat16)] * 2
        + [pltpu.VMEM((rows * size, window * size), jnp.bfloat16)] * 2,
        compiler_params=pltpu.CompilerParams(vmem_limit_bytes=60 * 1024 * 1024),
        name="first_step" if first else "second_step",
    )(columns, current, before, after)


def over_rows(x):
    count = lax.axis_size("row")
    stride = 1
    for length in (2, 4, count // 8):
        groups = [
            [base + k * stride for k in range(length)]
            for base in range(count)
            if (base // stride) % length == 0
        ]
        x = lax.psum(x, "row", axis_index_groups=groups)
        stride *= length
    return x


def on_device(density, block_columns):
    order_total = lax.axis_size("row") * density.shape[0] * density.shape[2]
    count = lax.axis_size("row")
    up = [(i, i + 1) for i in range(count - 1)]
    down = [(j, i) for i, j in up]
    low, high = edges(density, block_columns)
    before, after = lax.ppermute(high, "row", up), lax.ppermute(low, "row", down)
    current, low, high, early = step(True, block_columns, density, before, after)
    before, after = lax.ppermute(high, "row", up), lax.ppermute(low, "row", down)
    current, late = step(False, block_columns, current, before, after)
    traces = jnp.sum(over_rows(early + late), axis=1)[: STEPS + 1]
    return current, traces / order_total


def solution(mesh):
    in_specs = (P(("image", "row"), None, None, None), P(("image", "row"), None))
    out_specs = (P(("image", "row"), None, None, None), P("image"))
    return jax.shard_map(
        on_device, mesh=mesh, in_specs=in_specs, out_specs=out_specs, check_vma=False
    )
```

profile of v0, /device:TPU:46, one launch (start us, length us, event | category | flops | bytes accessed | tf_op | source)
XLA Modules:
  0.0 130.2 jit_solution(18264872672355983766)
XLA Ops:
  0.6 2.1 %edges.1 = (f32[6,128,128]{2,1,0:T(8,128)}, f32[6,128,128]{2,1,0:T(8,128)}) custom-call(s32[8,7]{1,0:T(8,128)} %columns_ref.5, f32[8,7,128,128]{3,2,1,0:T(8,128)} %p_ref.1, f32[8,7,128,128]{3,2,1,0:T(8,128)} %p_ref.1, f32[8,7,128,128]{3,2,1,0:T(8,128)} %p_ref.1, f32[8,7,128,128]{3,2,1,0:T(8,128)} %p_ref.1, f32[8,7,128,128]{3,2,1,0:T(8,128)} %p_ref.1, ...), custom_call_target="tpu_custom_call" | custom-call | tf_op jit(solution)/shard_map/edges/pallas_call | solution.py:44
  2.7 1.8 %collective-permute-start = (f32[6,128,128]{2,1,0:T(8,128)}, f32[6,128,128]{2,1,0:T(8,128)S(1)}, u32[]{:S(2)}, u32[]{:S(2)}) collective-permute-start(f32[6,128,128]{2,1,0:T(8,128)} %get-tuple-element.10), channel_id=1, source_target_pairs={{0,1},{1,2},{2,3},{3,4},{4,5},{5,6},{6,7},{7,8},{8,9},{9,10},{10,1... | collective-permute-start | bytes 1179656 | tf_op jit(solution)/shard_map/ppermute | solution.py:216
  4.6 1.3 %collective-permute-start.1 = (f32[6,128,128]{2,1,0:T(8,128)}, f32[6,128,128]{2,1,0:T(8,128)S(1)}, u32[]{:S(2)}, u32[]{:S(2)}) collective-permute-start(f32[6,128,128]{2,1,0:T(8,128)} %get-tuple-element.11), channel_id=1, source_target_pairs={{1,0},{2,1},{3,2},{4,3},{5,4},{6,5},{7,6},{8,7},{9,8},{10,9},{11,1... | collective-permute-start | bytes 1179656 | tf_op jit(solution)/shard_map/ppermute | solution.py:216
  5.9 0.2 collective-permute-done.before_ref
  6.1 0.0 copy-start.2
  6.1 4.2 %collective-permute-done.1.after_ref = f32[6,128,128]{2,1,0:T(8,128)S(1)} collective-permute-done((f32[6,128,128]{2,1,0:T(8,128)}, f32[6,128,128]{2,1,0:T(8,128)S(1)}, u32[]{:S(2)}, u32[]{:S(2)}) %collective-permute-start.1) | collective-permute-done | bytes 393248 | tf_op jit(solution)/shard_map/ppermute | solution.py:216
  10.2 0.0 copy-done.2
  10.2 0.0 copy-start.3
  10.2 0.7 copy-done.3
  11.0 18.1 %first_step.1 = (f32[8,7,128,128]{3,2,1,0:T(8,128)}, f32[15,128,128]{2,1,0:T(8,128)}, f32[15,128,128]{2,1,0:T(8,128)}, f32[8,128]{1,0:T(8,128)}) custom-call(s32[8,7]{1,0:T(8,128)} %columns_ref.5, f32[8,7,128,128]{3,2,1,0:T(8,128)} %p_ref.1, f32[6,128,128]{2,1,0:T(8,128)} %copy-done.2, f32[6,128,128]{2,1,0:T(8,128)} %copy-done.3), custom_call_target="tpu_custom_call" | custom-call | tf_op jit(solution)/shard_map/first_step/pallas_call | solution.py:184
  29.1 0.0 copy-start.4
  29.1 8.1 %collective-permute-start.2 = (f32[15,128,128]{2,1,0:T(8,128)}, f32[15,128,128]{2,1,0:T(8,128)S(1)}, u32[]{:S(2)}, u32[]{:S(2)}) collective-permute-start(f32[15,128,128]{2,1,0:T(8,128)} %get-tuple-element.13), channel_id=1, source_target_pairs={{0,1},{1,2},{2,3},{3,4},{4,5},{5,6},{6,7},{7,8},{8,9},{9,10},{10,1... | collective-permute-start | bytes 2949128 | tf_op jit(solution)/shard_map/ppermute | solution.py:218
  37.2 1.3 %collective-permute-start.3 = (f32[15,128,128]{2,1,0:T(8,128)}, f32[15,128,128]{2,1,0:T(8,128)S(1)}, u32[]{:S(2)}, u32[]{:S(2)}) collective-permute-start(f32[15,128,128]{2,1,0:T(8,128)} %get-tuple-element.14), channel_id=1, source_target_pairs={{1,0},{2,1},{3,2},{4,3},{5,4},{6,5},{7,6},{8,7},{9,8},{10,9},{11,1... | collective-permute-start | bytes 2949128 | tf_op jit(solution)/shard_map/ppermute | solution.py:218
  38.5 1.0 collective-permute-done.2.before_ref
  39.6 0.0 copy-start
  39.6 2.4 %collective-permute-done.3.after_ref = f32[15,128,128]{2,1,0:T(8,128)S(1)} collective-permute-done((f32[15,128,128]{2,1,0:T(8,128)}, f32[15,128,128]{2,1,0:T(8,128)S(1)}, u32[]{:S(2)}, u32[]{:S(2)}) %collective-permute-start.3) | collective-permute-done | bytes 983072 | tf_op jit(solution)/shard_map/ppermute | solution.py:218
  41.9 0.0 copy-start.1
  41.9 0.0 copy-done
  41.9 1.0 copy-done.1
  42.9 17.6 %second_step.1 = (f32[8,7,128,128]{3,2,1,0:T(8,128)}, f32[8,128]{1,0:T(8,128)}) custom-call(s32[8,7]{1,0:T(8,128)} %columns_ref.5, f32[8,7,128,128]{3,2,1,0:T(8,128)} %get-tuple-element.12.p_ref, f32[15,128,128]{2,1,0:T(8,128)} %copy-done, f32[15,128,128]{2,1,0:T(8,128)} %copy-done.1), custom_call_target="tpu_custom_call" | custom-call | tf_op jit(solution)/shard_map/second_step/pallas_call | solution.py:184
  60.5 0.0 copy-done.4
  60.5 0.7 add.9
  61.2 13.5 %psum.21 = f32[8,128]{1,0:T(8,128)S(1)} all-reduce(f32[8,128]{1,0:T(8,128)S(1)} %add.9), channel_id=1, replica_groups={{0,1},{2,3},{4,5},{6,7},{8,9},{10,11},{12,13},{14,15},{16,17},{18,19},{..., use_global_device_ids=true, to_apply=%region_0.0 | all-reduce | flops 1024 | bytes 8192 | tf_op jit(solution)/shard_map/psum | solution.py:205
  74.7 16.7 %psum.22 = f32[8,128]{1,0:T(8,128)S(1)} all-reduce(f32[8,128]{1,0:T(8,128)S(1)} %psum.21), channel_id=1, replica_groups={{0,2,4,6},{1,3,5,7},{8,10,12,14},{9,11,13,15},{16,18,20,22},{17,19,21,2..., use_global_device_ids=true, to_apply=%region_1.0 | all-reduce | flops 1024 | bytes 8192 | tf_op jit(solution)/shard_map/psum | solution.py:205
  91.4 38.1 %psum.23 = f32[8,128]{1,0:T(8,128)S(1)} all-reduce(f32[8,128]{1,0:T(8,128)S(1)} %psum.22), channel_id=1, replica_groups={{0,8,16,24,32,40,48,56},{1,9,17,25,33,41,49,57},{2,10,18,26,34,42,50,58..., use_global_device_ids=true, to_apply=%region_2.0 | all-reduce | flops 1024 | bytes 8192 | tf_op jit(solution)/shard_map/psum | solution.py:205
  129.5 0.1 reduce_sum.9
  129.6 0.5 slice_multiply_fusion
Async XLA Ops:
  2.7 3.4 %collective-permute-start = (f32[6,128,128]{2,1,0:T(8,128)}, f32[6,128,128]{2,1,0:T(8,128)S(1)}, u32[]{:S(2)}, u32[]{:S(2)}) collective-permute-start(f32[6,128,128]{2,1,0:T(8,128)} %get-tuple-element.10), channel_id=1, source_target_pairs={{0,1},{1,2},{2,3},{3,4},{4,5},{5,6},{6,7},{7,8},{8,9},{9,10},{10,1... | collective-permute-start | bytes 1179656 | tf_op jit(solution)/shard_map/ppermute | solution.py:216
  4.6 5.7 %collective-permute-start.1 = (f32[6,128,128]{2,1,0:T(8,128)}, f32[6,128,128]{2,1,0:T(8,128)S(1)}, u32[]{:S(2)}, u32[]{:S(2)}) collective-permute-start(f32[6,128,128]{2,1,0:T(8,128)} %get-tuple-element.11), channel_id=1, source_target_pairs={{1,0},{2,1},{3,2},{4,3},{5,4},{6,5},{7,6},{8,7},{9,8},{10,9},{11,1... | collective-permute-start | bytes 1179656 | tf_op jit(solution)/shard_map/ppermute | solution.py:216
  6.1 4.2 %copy-start.2 = (f32[6,128,128]{2,1,0:T(8,128)}, f32[6,128,128]{2,1,0:T(8,128)S(1)}, u32[]{:S(2)}) copy-start(f32[6,128,128]{2,1,0:T(8,128)S(1)} %collective-permute-done.before_ref) | copy-start | bytes 1179652
  10.2 0.7 copy-start.3
  29.1 31.4 %copy-start.4 = (f32[8,128]{1,0:T(8,128)S(1)}, f32[8,128]{1,0:T(8,128)}, u32[]{:S(2)}) copy-start(f32[8,128]{1,0:T(8,128)} %get-tuple-element.16) | copy-start | bytes 12292
  29.1 10.4 %collective-permute-start.2 = (f32[15,128,128]{2,1,0:T(8,128)}, f32[15,128,128]{2,1,0:T(8,128)S(1)}, u32[]{:S(2)}, u32[]{:S(2)}) collective-permute-start(f32[15,128,128]{2,1,0:T(8,128)} %get-tuple-element.13), channel_id=1, source_target_pairs={{0,1},{1,2},{2,3},{3,4},{4,5},{5,6},{6,7},{7,8},{8,9},{9,10},{10,1... | collective-permute-start | bytes 2949128 | tf_op jit(solution)/shard_map/ppermute | solution.py:218
  37.2 4.7 %collective-permute-start.3 = (f32[15,128,128]{2,1,0:T(8,128)}, f32[15,128,128]{2,1,0:T(8,128)S(1)}, u32[]{:S(2)}, u32[]{:S(2)}) collective-permute-start(f32[15,128,128]{2,1,0:T(8,128)} %get-tuple-element.14), channel_id=1, source_target_pairs={{1,0},{2,1},{3,2},{4,3},{5,4},{6,5},{7,6},{8,7},{9,8},{10,9},{11,1... | collective-permute-start | bytes 2949128 | tf_op jit(solution)/shard_map/ppermute | solution.py:218
  39.6 2.4 %copy-start = (f32[15,128,128]{2,1,0:T(8,128)}, f32[15,128,128]{2,1,0:T(8,128)S(1)}, u32[]{:S(2)}) copy-start(f32[15,128,128]{2,1,0:T(8,128)S(1)} %collective-permute-done.2.before_ref) | copy-start | bytes 2949124
  41.9 1.0 copy-start.1
where the time goes:
time: 131 us; the launch traced here: 130 us
  blocking collectives  68.3 us (52%)
  Pallas kernels  37.8 us (29%)
  starting transfers between devices  12.6 us (10%)
  waiting for transfers between devices  7.74 us (6%)
  local copies, waits for them, and re-layouts  1.74 us (1%)
  other arithmetic  1.31 us (1%)
    psum x3, blocking collectives, over_rows(): x = lax.psum(x, 'row', axis_index_groups=groups)  68.3 us
    pallas_call x2, Pallas kernels, step(): pl.pallas_call(functools.partial(step_kernel, first), in_specs=[pl.BlockS...  35.7 us
    ppermute x2, starting transfers between devices, on_device(): lax.ppermute(high, 'row', up)  9.95 us
    ppermute x2, waiting for transfers between devices, on_device(): lax.ppermute(low, 'row', down)  6.53 us
  transfers between devices with their start and end apart: 4, of which 4 were waited for; matrix products, arithmetic and copies ran while one was open for 0% of the time, Pallas kernels for 0%

commit v1 on v0

--- a/solution.py
+++ b/solution.py
@@ -57,13 +57,13 @@
     return jnp.sum(jnp.where(eye, block, 0.0), axis=0, keepdims=True)
 
 
-def step_kernel(first, columns_ref, p_ref, before_ref, after_ref, out_ref, *rest):
+def step_kernel(first, columns_ref, p_ref, before_ref, after_ref, *rest):
+    if first:
+        out_ref, low_ref, high_ref, trace_ref, dh, dl, sh, sl = rest
+    else:
+        early_ref, out_hbm, trace_ref, out_ref, dh, dl, sh, sl, out_sems = rest
     rows, slots, size, _ = p_ref.shape
     window = rows + 2 * PAD
-    if first:
-        low_ref, high_ref, trace_ref, dh, dl, sh, sl = rest
-    else:
-        trace_ref, dh, dl, sh, sl = rest
 
     def keep(i, s):
         return (columns_ref[i, s] >= 0).astype(jnp.float32)
@@ -76,30 +76,39 @@
         area(dh, p, q)[...] = high
         area(dl, p, q)[...] = low
 
-    filled = set()
+    zero = jnp.zeros((size, size), jnp.bfloat16)
+    last = PAD + rows + HALF
+    for p in range(window):
+        for q in range(window):
+            inside = PAD - HALF <= min(p, q) and max(p, q) < last and abs(p - q) <= HALF
+            if abs(p // 2 - q // 2) <= 2 and not inside:
+                area(dh, p, q)[...] = zero
+                area(dl, p, q)[...] = zero
+    for i in range(rows):
+        for q in range(window):
+            if abs((PAD + i) // 2 - q // 2) <= 2 and abs(PAD + i - q) > HALF:
+                area(sh, i, q)[...] = zero
+                area(sl, i, q)[...] = zero
+
     old_trace = jnp.zeros((1, size), jnp.float32)
     for i in range(rows):
         for s in range(slots):
             block = p_ref[i, s]
             if first:
                 block = block * keep(i, s)
-            if s == HALF:
-                old_trace += diagonal_lanes(block)
+                if s == HALF:
+                    old_trace += diagonal_lanes(block)
             p, q = PAD + i, PAD + i + s - HALF
             put(p, q, block)
-            filled.add((p, q))
             if first and not PAD <= q < PAD + rows:
                 put(q, p, block.T)
-                filled.add((q, p))
     if first:
         for ref, base in ((before_ref, PAD - HALF), (after_ref, PAD + rows)):
             for n, (a, b) in enumerate(TRIANGLE):
                 block = ref[n]
                 put(base + a, base + b, block)
-                filled.add((base + a, base + b))
                 if a != b:
                     put(base + b, base + a, block.T)
-                    filled.add((base + b, base + a))
     else:
         for ref, picks, shift in (
             (before_ref, high_edge(rows), PAD - rows),
@@ -108,20 +117,8 @@
             for n, (i, s) in enumerate(picks):
                 p = i + shift
                 put(p, p + s - HALF, ref[n])
-                filled.add((p, p + s - HALF))
-    zero = jnp.zeros((size, size), jnp.bfloat16)
-    for p in range(window):
-        for q in range(window):
-            if abs(p // 2 - q // 2) <= 2 and (p, q) not in filled:
-                area(dh, p, q)[...] = zero
-                area(dl, p, q)[...] = zero
-    for i in range(rows):
-        for q in range(window):
-            if abs((PAD + i) // 2 - q // 2) <= 2 and abs(PAD + i - q) > HALF:
-                area(sh, i, q)[...] = zero
-                area(sl, i, q)[...] = zero
-
-    def product(xh, xl, shift, write):
+
+    def product(xh, xl, shift, write, leave):
         for i in range(rows):
             p = PAD + i
             first_pair, last_pair = (p - HALF) // 2, (p + HALF) // 2
@@ -142,6 +139,8 @@
                     s = 2 * pair + half - p + HALF
                     if 0 <= s < slots:
                         write(i, s, total[:, half * size : (half + 1) * size] * keep(i, s))
+            if i:
+                leave(i - 1)
 
     def write_square(i, s, block):
         out_ref[i, s] = block
@@ -149,7 +148,7 @@
         area(sh, i, PAD + i + s - HALF)[...] = high
         area(sl, i, PAD + i + s - HALF)[...] = low
 
-    product(dh, dl, PAD, write_square)
+    product(dh, dl, PAD, write_square, lambda i: None)
     traces = []
 
     def write_next(i, s, cube):
@@ -157,40 +156,59 @@
         out_ref[i, s] = block
         if s == HALF:
             traces.append(diagonal_lanes(block))
+
+    leaving = []
+
+    def leave(i):
         if first:
-            for ref, picks in ((low_ref, low_edge()), (high_ref, high_edge(rows))):
-                if (i, s) in picks:
-                    ref[picks.index((i, s))] = block
-
-    product(sh, sl, 0, write_next)
+            for edge_ref, picks in ((low_ref, low_edge()), (high_ref, high_edge(rows))):
+                for n, (row, s) in enumerate(picks):
+                    if row == i:
+                        edge_ref[n] = out_ref[i, s]
+            return
+        copy = pltpu.make_async_copy(out_ref.at[i], out_hbm.at[i], out_sems.at[i])
+        copy.start()
+        leaving.append(copy)
+
+    product(sh, sl, 0, write_next, leave)
     new_trace = sum(traces[1:], traces[0])
-    trace_ref[...] = jnp.zeros(trace_ref.shape, jnp.float32)
-    if first:
+    if first:
+        trace_ref[...] = jnp.zeros(trace_ref.shape, jnp.float32)
         trace_ref[0:1, :] = old_trace
         trace_ref[1:2, :] = new_trace
     else:
+        trace_ref[...] = early_ref[...]
         trace_ref[2:3, :] = new_trace
-
-
-def step(first, columns, current, before, after):
+    leave(rows - 1)
+    for copy in leaving:
+        copy.wait()
+
+
+def step(first, columns, current, before, after, early=None):
     rows, slots, size, _ = current.shape
     window = rows + 2 * PAD
     f32 = jnp.float32
-    outs = [jax.ShapeDtypeStruct(current.shape, f32)]
-    if first:
-        outs += [jax.ShapeDtypeStruct((len(low_edge()), size, size), f32)] * 2
-    outs += [jax.ShapeDtypeStruct((8, size), f32)]
     vmem = pl.BlockSpec(memory_space=pltpu.VMEM)
+    dense = [pltpu.VMEM((window * size, window * size), jnp.bfloat16)] * 2
+    dense += [pltpu.VMEM((rows * size, window * size), jnp.bfloat16)] * 2
+    traces = jax.ShapeDtypeStruct((8, size), f32)
+    if first:
+        edge = jax.ShapeDtypeStruct((len(low_edge()), size, size), f32)
+        outs, out_specs = [jax.ShapeDtypeStruct(current.shape, f32), edge, edge, traces], [vmem] * 4
+        scratch = dense
+    else:
+        outs = [jax.ShapeDtypeStruct(current.shape, f32), traces]
+        out_specs = [pl.BlockSpec(memory_space=pl.ANY), vmem]
+        scratch = [pltpu.VMEM(current.shape, f32)] + dense + [pltpu.SemaphoreType.DMA((rows,))]
     return pl.pallas_call(
         functools.partial(step_kernel, first),
-        in_specs=[pl.BlockSpec(memory_space=pltpu.SMEM), vmem, vmem, vmem],
-        out_specs=[vmem] * len(outs),
+        in_specs=[pl.BlockSpec(memory_space=pltpu.SMEM)] + [vmem] * (3 if first else 4),
+        out_specs=out_specs,
         out_shape=outs,
-        scratch_shapes=[pltpu.VMEM((window * size, window * size), jnp.bfloat16)] * 2
-        + [pltpu.VMEM((rows * size, window * size), jnp.bfloat16)] * 2,
-        compiler_params=pltpu.CompilerParams(vmem_limit_bytes=60 * 1024 * 1024),
+        scratch_shapes=scratch,
+        compiler_params=pltpu.CompilerParams(vmem_limit_bytes=44 * 1024 * 1024),
         name="first_step" if first else "second_step",
-    )(columns, current, before, after)
+    )(columns, current, before, after, *([] if first else [early]))
 
 
 def over_rows(x):
@@ -216,8 +234,8 @@
     before, after = lax.ppermute(high, "row", up), lax.ppermute(low, "row", down)
     current, low, high, early = step(True, block_columns, density, before, after)
     before, after = lax.ppermute(high, "row", up), lax.ppermute(low, "row", down)
-    current, late = step(False, block_columns, current, before, after)
-    traces = jnp.sum(over_rows(early + late), axis=1)[: STEPS + 1]
+    current, traces = step(False, block_columns, current, before, after, early)
+    traces = jnp.sum(over_rows(traces), axis=1)[: STEPS + 1]
     return current, traces / order_total
 
 

time: 131 us -> 124 us (0.947)
  Pallas kernels: 37.8 us -> 31.4 us
    pallas_call x2, Pallas kernels: 35.7 us -> 29.4 us  [step(): pl.pallas_call(functools.partial(step_kernel, first), in_specs=[pl.BlockS...]
where the time goes in v1:
time: 124 us; the launch traced here: 123 us
  blocking collectives  68.4 us (55%)
  Pallas kernels  31.4 us (25%)
  starting transfers between devices  12.4 us (10%)
  waiting for transfers between devices  7.53 us (6%)
  local copies, waits for them, and re-layouts  2.04 us (2%)
    psum x3, blocking collectives, over_rows(): x = lax.psum(x, 'row', axis_index_groups=groups)  68.4 us
    pallas_call x2, Pallas kernels, step(): pl.pallas_call(functools.partial(step_kernel, first), in_specs=[pl.BlockS...  29.4 us
    ppermute x2, starting transfers between devices, on_device(): lax.ppermute(high, 'row', up)  9.82 us
    ppermute x2, waiting for transfers between devices, on_device(): lax.ppermute(low, 'row', down)  6.53 us
    ppermute x2, starting transfers between devices, on_device(): lax.ppermute(low, 'row', down)  2.62 us
  transfers between devices with their start and end apart: 4, of which 4 were waited for; matrix products, arithmetic and copies ran while one was open for 0% of the time, Pallas kernels for 0%

profile of v1, /device:TPU:46, one launch (start us, length us, event | category | flops | bytes accessed | tf_op | source)
XLA Modules:
  0.0 123.2 jit_solution(17234185484689283103)
XLA Ops:
  0.6 0.0 copy-start.1
  0.6 2.1 %edges.1 = (f32[6,128,128]{2,1,0:T(8,128)}, f32[6,128,128]{2,1,0:T(8,128)}) custom-call(s32[8,7]{1,0:T(8,128)} %columns_ref.5, f32[8,7,128,128]{3,2,1,0:T(8,128)} %p_ref.1, f32[8,7,128,128]{3,2,1,0:T(8,128)} %p_ref.1, f32[8,7,128,128]{3,2,1,0:T(8,128)} %p_ref.1, f32[8,7,128,128]{3,2,1,0:T(8,128)} %p_ref.1, f32[8,7,128,128]{3,2,1,0:T(8,128)} %p_ref.1, ...), custom_call_target="tpu_custom_call" | custom-call | tf_op jit(solution)/shard_map/edges/pallas_call | solution.py:44
  2.7 1.8 %collective-permute-start = (f32[6,128,128]{2,1,0:T(8,128)}, f32[6,128,128]{2,1,0:T(8,128)S(1)}, u32[]{:S(2)}, u32[]{:S(2)}) collective-permute-start(f32[6,128,128]{2,1,0:T(8,128)} %get-tuple-element.10), channel_id=1, source_target_pairs={{0,1},{1,2},{2,3},{3,4},{4,5},{5,6},{6,7},{7,8},{8,9},{9,10},{10,1... | collective-permute-start | bytes 1179656 | tf_op jit(solution)/shard_map/ppermute | solution.py:234
  4.6 1.3 %collective-permute-start.1 = (f32[6,128,128]{2,1,0:T(8,128)}, f32[6,128,128]{2,1,0:T(8,128)S(1)}, u32[]{:S(2)}, u32[]{:S(2)}) collective-permute-start(f32[6,128,128]{2,1,0:T(8,128)} %get-tuple-element.11), channel_id=1, source_target_pairs={{1,0},{2,1},{3,2},{4,3},{5,4},{6,5},{7,6},{8,7},{9,8},{10,9},{11,1... | collective-permute-start | bytes 1179656 | tf_op jit(solution)/shard_map/ppermute | solution.py:234
  5.9 0.2 collective-permute-done.before_ref
  6.1 4.2 %collective-permute-done.1.after_ref = f32[6,128,128]{2,1,0:T(8,128)S(1)} collective-permute-done((f32[6,128,128]{2,1,0:T(8,128)}, f32[6,128,128]{2,1,0:T(8,128)S(1)}, u32[]{:S(2)}, u32[]{:S(2)}) %collective-permute-start.1) | collective-permute-done | bytes 393248 | tf_op jit(solution)/shard_map/ppermute | solution.py:234
  10.2 0.0 copy-done.1
  10.2 0.0 copy-start
  10.2 2.0 %copy-done = f32[8,7,128,128]{3,2,1,0:T(8,128)S(1)} copy-done((f32[8,7,128,128]{3,2,1,0:T(8,128)S(1)}, f32[8,7,128,128]{3,2,1,0:T(8,128)}, u32[]{:S(2)}) %copy-start) | copy-done | bytes 3670040
  12.3 14.4 %first_step.1 = (f32[8,7,128,128]{3,2,1,0:T(8,128)S(1)}, f32[15,128,128]{2,1,0:T(8,128)S(1)}, f32[15,128,128]{2,1,0:T(8,128)S(1)}, f32[8,128]{1,0:T(8,128)S(1)}) custom-call(s32[8,7]{1,0:T(8,128)S(1)} %copy-done.1, f32[8,7,128,128]{3,2,1,0:T(8,128)S(1)} %copy-done, f32[6,128,128]{2,1,0:T(8,128)S(1)} %collective-permute-done.before_ref, ...), custom_call_target="tpu_custom_call" | custom-call | tf_op jit(solution)/shard_map/first_step/pallas_call | solution.py:203
  26.7 8.0 %collective-permute-start.2 = (f32[15,128,128]{2,1,0:T(8,128)S(1)}, f32[15,128,128]{2,1,0:T(8,128)S(1)}, u32[]{:S(2)}, u32[]{:S(2)}) collective-permute-start(f32[15,128,128]{2,1,0:T(8,128)S(1)} %get-tuple-element.13), channel_id=1, source_target_pairs={{0,1},{1,2},{2,3},{3,4},{4,5},{5,6},{6,7},{7,8},{8,9},{9,10},{10,1... | collective-permute-start | bytes 2949128 | tf_op jit(solution)/shard_map/ppermute | solution.py:236
  34.7 1.3 %collective-permute-start.3 = (f32[15,128,128]{2,1,0:T(8,128)S(1)}, f32[15,128,128]{2,1,0:T(8,128)S(1)}, u32[]{:S(2)}, u32[]{:S(2)}) collective-permute-start(f32[15,128,128]{2,1,0:T(8,128)S(1)} %get-tuple-element.14), channel_id=1, source_target_pairs={{1,0},{2,1},{3,2},{4,3},{5,4},{6,5},{7,6},{8,7},{9,8},{10,9},{11,1... | collective-permute-start | bytes 2949128 | tf_op jit(solution)/shard_map/ppermute | solution.py:236
  36.0 0.8 collective-permute-done.2.before_ref
  36.8 2.4 %collective-permute-done.3.after_ref = f32[15,128,128]{2,1,0:T(8,128)S(1)} collective-permute-done((f32[15,128,128]{2,1,0:T(8,128)S(1)}, f32[15,128,128]{2,1,0:T(8,128)S(1)}, u32[]{:S(2)}, u32[]{:S(2)}) %collective-permute-start.3) | collective-permute-done | bytes 983072 | tf_op jit(solution)/shard_map/ppermute | solution.py:236
  39.2 15.0 %second_step.1 = (f32[8,7,128,128]{3,2,1,0:T(8,128)}, f32[8,128]{1,0:T(8,128)S(1)}) custom-call(s32[8,7]{1,0:T(8,128)S(1)} %copy-done.1, f32[8,7,128,128]{3,2,1,0:T(8,128)S(1)} %get-tuple-element.12.p_ref, f32[15,128,128]{2,1,0:T(8,128)S(1)} %collective-permute-done.2.before_ref, f32[15,128,128]{2,1,0:T(8,128)S(1)} %collective-permute-done.3.after_ref, ...), custom_call_target="tpu_custom_call" | custom-call | tf_op jit(solution)/shard_map/second_step/pallas_call | solution.py:203
  54.1 13.6 %psum.21 = f32[8,128]{1,0:T(8,128)S(1)} all-reduce(f32[8,128]{1,0:T(8,128)S(1)} %get-tuple-element.17), channel_id=1, replica_groups={{0,1},{2,3},{4,5},{6,7},{8,9},{10,11},{12,13},{14,15},{16,17},{18,19},{..., use_global_device_ids=true, to_apply=%region_0.0 | all-reduce | flops 1024 | bytes 8192 | tf_op jit(solution)/shard_map/psum | solution.py:223
  67.7 16.7 %psum.22 = f32[8,128]{1,0:T(8,128)S(1)} all-reduce(f32[8,128]{1,0:T(8,128)S(1)} %psum.21), channel_id=1, replica_groups={{0,2,4,6},{1,3,5,7},{8,10,12,14},{9,11,13,15},{16,18,20,22},{17,19,21,2..., use_global_device_ids=true, to_apply=%region_1.0 | all-reduce | flops 1024 | bytes 8192 | tf_op jit(solution)/shard_map/psum | solution.py:223
  84.5 38.1 %psum.23 = f32[8,128]{1,0:T(8,128)S(1)} all-reduce(f32[8,128]{1,0:T(8,128)S(1)} %psum.22), channel_id=1, replica_groups={{0,8,16,24,32,40,48,56},{1,9,17,25,33,41,49,57},{2,10,18,26,34,42,50,58..., use_global_device_ids=true, to_apply=%region_2.0 | all-reduce | flops 1024 | bytes 8192 | tf_op jit(solution)/shard_map/psum | solution.py:223
  122.5 0.1 reduce_sum.9
  122.7 0.5 slice_multiply_fusion
Async XLA Ops:
  0.6 9.6 %copy-start.1 = (s32[8,7]{1,0:T(8,128)S(1)}, s32[8,7]{1,0:T(8,128)}, u32[]{:S(2)}) copy-start(s32[8,7]{1,0:T(8,128)} %columns_ref.5) | copy-start | bytes 676
  2.7 3.4 %collective-permute-start = (f32[6,128,128]{2,1,0:T(8,128)}, f32[6,128,128]{2,1,0:T(8,128)S(1)}, u32[]{:S(2)}, u32[]{:S(2)}) collective-permute-start(f32[6,128,128]{2,1,0:T(8,128)} %get-tuple-element.10), channel_id=1, source_target_pairs={{0,1},{1,2},{2,3},{3,4},{4,5},{5,6},{6,7},{7,8},{8,9},{9,10},{10,1... | collective-permute-start | bytes 1179656 | tf_op jit(solution)/shard_map/ppermute | solution.py:234
  4.6 5.7 %collective-permute-start.1 = (f32[6,128,128]{2,1,0:T(8,128)}, f32[6,128,128]{2,1,0:T(8,128)S(1)}, u32[]{:S(2)}, u32[]{:S(2)}) collective-permute-start(f32[6,128,128]{2,1,0:T(8,128)} %get-tuple-element.11), channel_id=1, source_target_pairs={{1,0},{2,1},{3,2},{4,3},{5,4},{6,5},{7,6},{8,7},{9,8},{10,9},{11,1... | collective-permute-start | bytes 1179656 | tf_op jit(solution)/shard_map/ppermute | solution.py:234
  10.2 2.0 %copy-start = (f32[8,7,128,128]{3,2,1,0:T(8,128)S(1)}, f32[8,7,128,128]{3,2,1,0:T(8,128)}, u32[]{:S(2)}) copy-start(f32[8,7,128,128]{3,2,1,0:T(8,128)} %p_ref.1) | copy-start | bytes 11010052
  26.7 10.1 %collective-permute-start.2 = (f32[15,128,128]{2,1,0:T(8,128)S(1)}, f32[15,128,128]{2,1,0:T(8,128)S(1)}, u32[]{:S(2)}, u32[]{:S(2)}) collective-permute-start(f32[15,128,128]{2,1,0:T(8,128)S(1)} %get-tuple-element.13), channel_id=1, source_target_pairs={{0,1},{1,2},{2,3},{3,4},{4,5},{5,6},{6,7},{7,8},{8,9},{9,10},{10,1... | collective-permute-start | bytes 2949128 | tf_op jit(solution)/shard_map/ppermute | solution.py:236
  34.7 4.5 %collective-permute-start.3 = (f32[15,128,128]{2,1,0:T(8,128)S(1)}, f32[15,128,128]{2,1,0:T(8,128)S(1)}, u32[]{:S(2)}, u32[]{:S(2)}) collective-permute-start(f32[15,128,128]{2,1,0:T(8,128)S(1)} %get-tuple-element.14), channel_id=1, source_target_pairs={{1,0},{2,1},{3,2},{4,3},{5,4},{6,5},{7,6},{8,7},{9,8},{10,9},{11,1... | collective-permute-start | bytes 2949128 | tf_op jit(solution)/shard_map/ppermute | solution.py:236

commit v2 on v1

--- a/solution.py
+++ b/solution.py
@@ -213,15 +213,13 @@
 
 def over_rows(x):
     count = lax.axis_size("row")
-    stride = 1
-    for length in (2, 4, count // 8):
+    for length, stride in ((count // 8, 8), (4, 2), (2, 1)):
         groups = [
             [base + k * stride for k in range(length)]
             for base in range(count)
             if (base // stride) % length == 0
         ]
         x = lax.psum(x, "row", axis_index_groups=groups)
-        stride *= length
     return x
 
 

time: 124 us -> 122 us (0.984)
  blocking collectives: 68.4 us -> 65.7 us
    psum x3, blocking collectives: 68.4 us -> 65.7 us  [over_rows(): x = lax.psum(x, 'row', axis_index_groups=groups)]
where the time goes in v2:
time: 122 us; the launch traced here: 120 us
  blocking collectives  65.7 us (54%)
  Pallas kernels  31.4 us (26%)
  starting transfers between devices  12.4 us (10%)
  waiting for transfers between devices  7.53 us (6%)
  local copies, waits for them, and re-layouts  2.04 us (2%)
    psum x3, blocking collectives, over_rows(): x = lax.psum(x, 'row', axis_index_groups=groups)  65.7 us
    pallas_call x2, Pallas kernels, step(): pl.pallas_call(functools.partial(step_kernel, first), in_specs=[pl.BlockS...  29.4 us
    ppermute x2, starting transfers between devices, on_device(): lax.ppermute(high, 'row', up)  9.82 us
    ppermute x2, waiting for transfers between devices, on_device(): lax.ppermute(low, 'row', down)  6.53 us
    ppermute x2, starting transfers between devices, on_device(): lax.ppermute(low, 'row', down)  2.62 us
  transfers between devices with their start and end apart: 4, of which 4 were waited for; matrix products, arithmetic and copies ran while one was open for 0% of the time, Pallas kernels for 0%

profile of v2, /device:TPU:46, one launch (start us, length us, event | category | flops | bytes accessed | tf_op | source)
XLA Modules:
  0.0 120.4 jit_solution(15706516306575948759)
XLA Ops:
  0.6 0.0 copy-start.1
  0.6 2.1 %edges.1 = (f32[6,128,128]{2,1,0:T(8,128)}, f32[6,128,128]{2,1,0:T(8,128)}) custom-call(s32[8,7]{1,0:T(8,128)} %columns_ref.5, f32[8,7,128,128]{3,2,1,0:T(8,128)} %p_ref.1, f32[8,7,128,128]{3,2,1,0:T(8,128)} %p_ref.1, f32[8,7,128,128]{3,2,1,0:T(8,128)} %p_ref.1, f32[8,7,128,128]{3,2,1,0:T(8,128)} %p_ref.1, f32[8,7,128,128]{3,2,1,0:T(8,128)} %p_ref.1, ...), custom_call_target="tpu_custom_call" | custom-call | tf_op jit(solution)/shard_map/edges/pallas_call | solution.py:44
  2.7 1.8 %collective-permute-start = (f32[6,128,128]{2,1,0:T(8,128)}, f32[6,128,128]{2,1,0:T(8,128)S(1)}, u32[]{:S(2)}, u32[]{:S(2)}) collective-permute-start(f32[6,128,128]{2,1,0:T(8,128)} %get-tuple-element.10), channel_id=1, source_target_pairs={{0,1},{1,2},{2,3},{3,4},{4,5},{5,6},{6,7},{7,8},{8,9},{9,10},{10,1... | collective-permute-start | bytes 1179656 | tf_op jit(solution)/shard_map/ppermute | solution.py:232
  4.6 1.3 %collective-permute-start.1 = (f32[6,128,128]{2,1,0:T(8,128)}, f32[6,128,128]{2,1,0:T(8,128)S(1)}, u32[]{:S(2)}, u32[]{:S(2)}) collective-permute-start(f32[6,128,128]{2,1,0:T(8,128)} %get-tuple-element.11), channel_id=1, source_target_pairs={{1,0},{2,1},{3,2},{4,3},{5,4},{6,5},{7,6},{8,7},{9,8},{10,9},{11,1... | collective-permute-start | bytes 1179656 | tf_op jit(solution)/shard_map/ppermute | solution.py:232
  5.9 0.2 collective-permute-done.before_ref
  6.1 4.2 %collective-permute-done.1.after_ref = f32[6,128,128]{2,1,0:T(8,128)S(1)} collective-permute-done((f32[6,128,128]{2,1,0:T(8,128)}, f32[6,128,128]{2,1,0:T(8,128)S(1)}, u32[]{:S(2)}, u32[]{:S(2)}) %collective-permute-start.1) | collective-permute-done | bytes 393248 | tf_op jit(solution)/shard_map/ppermute | solution.py:232
  10.2 0.0 copy-done.1
  10.2 0.0 copy-start
  10.2 2.0 %copy-done = f32[8,7,128,128]{3,2,1,0:T(8,128)S(1)} copy-done((f32[8,7,128,128]{3,2,1,0:T(8,128)S(1)}, f32[8,7,128,128]{3,2,1,0:T(8,128)}, u32[]{:S(2)}) %copy-start) | copy-done | bytes 3670040
  12.3 14.4 %first_step.1 = (f32[8,7,128,128]{3,2,1,0:T(8,128)S(1)}, f32[15,128,128]{2,1,0:T(8,128)S(1)}, f32[15,128,128]{2,1,0:T(8,128)S(1)}, f32[8,128]{1,0:T(8,128)S(1)}) custom-call(s32[8,7]{1,0:T(8,128)S(1)} %copy-done.1, f32[8,7,128,128]{3,2,1,0:T(8,128)S(1)} %copy-done, f32[6,128,128]{2,1,0:T(8,128)S(1)} %collective-permute-done.before_ref, ...), custom_call_target="tpu_custom_call" | custom-call | tf_op jit(solution)/shard_map/first_step/pallas_call | solution.py:203
  26.7 8.0 %collective-permute-start.2 = (f32[15,128,128]{2,1,0:T(8,128)S(1)}, f32[15,128,128]{2,1,0:T(8,128)S(1)}, u32[]{:S(2)}, u32[]{:S(2)}) collective-permute-start(f32[15,128,128]{2,1,0:T(8,128)S(1)} %get-tuple-element.13), channel_id=1, source_target_pairs={{0,1},{1,2},{2,3},{3,4},{4,5},{5,6},{6,7},{7,8},{8,9},{9,10},{10,1... | collective-permute-start | bytes 2949128 | tf_op jit(solution)/shard_map/ppermute | solution.py:234
  34.7 1.3 %collective-permute-start.3 = (f32[15,128,128]{2,1,0:T(8,128)S(1)}, f32[15,128,128]{2,1,0:T(8,128)S(1)}, u32[]{:S(2)}, u32[]{:S(2)}) collective-permute-start(f32[15,128,128]{2,1,0:T(8,128)S(1)} %get-tuple-element.14), channel_id=1, source_target_pairs={{1,0},{2,1},{3,2},{4,3},{5,4},{6,5},{7,6},{8,7},{9,8},{10,9},{11,1... | collective-permute-start | bytes 2949128 | tf_op jit(solution)/shard_map/ppermute | solution.py:234
  36.0 0.8 collective-permute-done.2.before_ref
  36.8 2.4 %collective-permute-done.3.after_ref = f32[15,128,128]{2,1,0:T(8,128)S(1)} collective-permute-done((f32[15,128,128]{2,1,0:T(8,128)S(1)}, f32[15,128,128]{2,1,0:T(8,128)S(1)}, u32[]{:S(2)}, u32[]{:S(2)}) %collective-permute-start.3) | collective-permute-done | bytes 983072 | tf_op jit(solution)/shard_map/ppermute | solution.py:234
  39.2 15.0 %second_step.1 = (f32[8,7,128,128]{3,2,1,0:T(8,128)}, f32[8,128]{1,0:T(8,128)S(1)}) custom-call(s32[8,7]{1,0:T(8,128)S(1)} %copy-done.1, f32[8,7,128,128]{3,2,1,0:T(8,128)S(1)} %get-tuple-element.12.p_ref, f32[15,128,128]{2,1,0:T(8,128)S(1)} %collective-permute-done.2.before_ref, f32[15,128,128]{2,1,0:T(8,128)S(1)} %collective-permute-done.3.after_ref, ...), custom_call_target="tpu_custom_call" | custom-call | tf_op jit(solution)/shard_map/second_step/pallas_call | solution.py:203
  54.1 54.3 %psum.21 = f32[8,128]{1,0:T(8,128)S(1)} all-reduce(f32[8,128]{1,0:T(8,128)S(1)} %get-tuple-element.17), channel_id=1, replica_groups={{0,8,16,24,32,40,48,56},{1,9,17,25,33,41,49,57},{2,10,18,26,34,42,50,58..., use_global_device_ids=true, to_apply=%region_0.0 | all-reduce | flops 1024 | bytes 8192 | tf_op jit(solution)/shard_map/psum | solution.py:222
  108.4 8.9 %psum.22 = f32[8,128]{1,0:T(8,128)S(1)} all-reduce(f32[8,128]{1,0:T(8,128)S(1)} %psum.21), channel_id=1, replica_groups={{0,2,4,6},{1,3,5,7},{8,10,12,14},{9,11,13,15},{16,18,20,22},{17,19,21,2..., use_global_device_ids=true, to_apply=%region_1.0 | all-reduce | flops 1024 | bytes 8192 | tf_op jit(solution)/shard_map/psum | solution.py:222
  117.3 2.5 %psum.23 = f32[8,128]{1,0:T(8,128)S(1)} all-reduce(f32[8,128]{1,0:T(8,128)S(1)} %psum.22), channel_id=1, replica_groups={{0,1},{2,3},{4,5},{6,7},{8,9},{10,11},{12,13},{14,15},{16,17},{18,19},{..., use_global_device_ids=true, to_apply=%region_2.0 | all-reduce | flops 1024 | bytes 8192 | tf_op jit(solution)/shard_map/psum | solution.py:222
  119.8 0.1 reduce_sum.9
  119.9 0.5 slice_multiply_fusion
Async XLA Ops:
  0.6 9.6 %copy-start.1 = (s32[8,7]{1,0:T(8,128)S(1)}, s32[8,7]{1,0:T(8,128)}, u32[]{:S(2)}) copy-start(s32[8,7]{1,0:T(8,128)} %columns_ref.5) | copy-start | bytes 676
  2.7 3.4 %collective-permute-start = (f32[6,128,128]{2,1,0:T(8,128)}, f32[6,128,128]{2,1,0:T(8,128)S(1)}, u32[]{:S(2)}, u32[]{:S(2)}) collective-permute-start(f32[6,128,128]{2,1,0:T(8,128)} %get-tuple-element.10), channel_id=1, source_target_pairs={{0,1},{1,2},{2,3},{3,4},{4,5},{5,6},{6,7},{7,8},{8,9},{9,10},{10,1... | collective-permute-start | bytes 1179656 | tf_op jit(solution)/shard_map/ppermute | solution.py:232
  4.6 5.7 %collective-permute-start.1 = (f32[6,128,128]{2,1,0:T(8,128)}, f32[6,128,128]{2,1,0:T(8,128)S(1)}, u32[]{:S(2)}, u32[]{:S(2)}) collective-permute-start(f32[6,128,128]{2,1,0:T(8,128)} %get-tuple-element.11), channel_id=1, source_target_pairs={{1,0},{2,1},{3,2},{4,3},{5,4},{6,5},{7,6},{8,7},{9,8},{10,9},{11,1... | collective-permute-start | bytes 1179656 | tf_op jit(solution)/shard_map/ppermute | solution.py:232
  10.2 2.0 %copy-start = (f32[8,7,128,128]{3,2,1,0:T(8,128)S(1)}, f32[8,7,128,128]{3,2,1,0:T(8,128)}, u32[]{:S(2)}) copy-start(f32[8,7,128,128]{3,2,1,0:T(8,128)} %p_ref.1) | copy-start | bytes 11010052
  26.7 10.1 %collective-permute-start.2 = (f32[15,128,128]{2,1,0:T(8,128)S(1)}, f32[15,128,128]{2,1,0:T(8,128)S(1)}, u32[]{:S(2)}, u32[]{:S(2)}) collective-permute-start(f32[15,128,128]{2,1,0:T(8,128)S(1)} %get-tuple-element.13), channel_id=1, source_target_pairs={{0,1},{1,2},{2,3},{3,4},{4,5},{5,6},{6,7},{7,8},{8,9},{9,10},{10,1... | collective-permute-start | bytes 2949128 | tf_op jit(solution)/shard_map/ppermute | solution.py:234
  34.7 4.5 %collective-permute-start.3 = (f32[15,128,128]{2,1,0:T(8,128)S(1)}, f32[15,128,128]{2,1,0:T(8,128)S(1)}, u32[]{:S(2)}, u32[]{:S(2)}) collective-permute-start(f32[15,128,128]{2,1,0:T(8,128)S(1)} %get-tuple-element.14), channel_id=1, source_target_pairs={{1,0},{2,1},{3,2},{4,3},{5,4},{6,5},{7,6},{8,7},{9,8},{10,9},{11,1... | collective-permute-start | bytes 2949128 | tf_op jit(solution)/shard_map/ppermute | solution.py:234
